TPU v7x, 32 devices: a whole 2x2x4 slice. The times are simulated.
32 devices in a mesh: dp: 2 (over x), tp: 4 (over z), section: 4 (over y, core).
Axes of the slice: x: 2, y: 2, z: 4, core: 2. Of those that a mesh axis runs over, the one named last changes fastest.
Arguments:
- tokens: bfloat16 [256, 2304], P('dp', 'section'), may hold values from -6 to 6
- hidden_grad: bfloat16 [256, 18432], P('dp', ('tp', 'section')), may hold values from -6 to 6
- norm_gain: float32 [2304], replicated, may hold values from 0.5 to 1.5
- w_gate: bfloat16 [2304, 18432], P('dp', ('tp', 'section')), may hold values from -0.125 to 0.125
- w_up: bfloat16 [2304, 18432], P('dp', ('tp', 'section')), may hold values from -0.125 to 0.125
Outputs:
- grad_tokens: bfloat16 [256, 2304], P('dp', ('tp', 'section'))
- grad_gain: float32 [2304], P(('tp', 'section'))
- grad_gate: bfloat16 [2304, 18432], P('dp', ('tp', 'section'))
- grad_up: bfloat16 [2304, 18432], P('dp', ('tp', 'section'))
All inputs are finite; a program needn't handle non-finite values.
Results may differ from a plain program's by a relative error of at most 0.018.
Values may be sent and summed in bfloat16 or wider, within the bound.
A program may use at most 128 MiB of HBM per device.

v0:
```python
import jax
import jax.numpy as jnp
from jax import lax
from jax.sharding import PartitionSpec as P

D = 2304
epsilon = 1e-06


def gated_unit(gate, up):
    return jax.nn.gelu(gate, approximate=True) * up


def shards(tokens, hidden_grad, norm_gain, w_gate, w_up):
    rows_in = lax.all_gather(tokens, "section", axis=1, tiled=True)
    inputs = rows_in.astype(jnp.float32)
    inv_rms = lax.rsqrt(jnp.mean(inputs * inputs, axis=1) + epsilon)
    normed = (inputs * inv_rms[:, None] * norm_gain).astype(jnp.bfloat16)
    full_gate, full_up = (
        lax.all_gather(w_gate, "dp", axis=0, tiled=True),
        lax.all_gather(w_up, "dp", axis=0, tiled=True),
    )
    gate = jnp.dot(normed, full_gate, preferred_element_type=jnp.float32)
    up = jnp.dot(normed, full_up, preferred_element_type=jnp.float32)
    hidden, pull = jax.vjp(gated_unit, gate, up)
    d_gate, d_up = pull(hidden_grad.astype(jnp.float32))
    d_gate = d_gate.astype(jnp.bfloat16)
    d_up = d_up.astype(jnp.bfloat16)
    contract_cols = (((1,), (1,)), ((), ()))
    contract_rows = (((0,), (0,)), ((), ()))
    features = full_gate.shape[0]
    own_width = features // lax.axis_size(("tp", "section"))
    first = lax.dot_general(full_gate, d_gate, contract_cols, preferred_element_type=jnp.float32)
    second = lax.dot_general(full_up, d_up, contract_cols, preferred_element_type=jnp.float32)
    d_columns = lax.psum_scatter(
        (first + second).astype(jnp.bfloat16), ("tp", "section"), scatter_dimension=0, tiled=True
    ).astype(jnp.float32)
    d_normed = d_columns.T
    offset = lax.axis_index(("tp", "section")) * own_width
    own_inputs = lax.dynamic_slice_in_dim(inputs, offset, own_width, 1)
    own_gain = lax.dynamic_slice_in_dim(norm_gain, offset, own_width, 0)
    gain_part = jnp.sum(d_normed * own_inputs * inv_rms[:, None], axis=0)
    row_part = jnp.sum(own_inputs * own_gain * d_normed, axis=1)
    grad_gain = lax.psum(gain_part, "dp")
    row_sum = lax.psum(row_part, ("tp", "section"))
    grad_tokens = (
        inv_rms[:, None] * own_gain * d_normed - own_inputs * (inv_rms**3 * row_sum / D)[:, None]
    )
    block = w_gate.shape[0]
    fwidth = w_gate.shape[1]
    cols_normed = lax.all_to_all(normed, "dp", split_axis=1, concat_axis=0, tiled=True)
    per_device = normed.shape[0]
    empty = jnp.zeros((block, fwidth), jnp.float32)
    piece_gate = lax.all_gather(d_gate, "dp", axis=0, tiled=True)
    piece_up = lax.all_gather(d_up, "dp", axis=0, tiled=True)

    def one_block(index, running):
        inner = index * per_device
        block_normed = lax.dynamic_slice_in_dim(cols_normed, inner, per_device, 0)
        block_gate = lax.dynamic_slice_in_dim(piece_gate, inner, per_device, 0)
        block_up = lax.dynamic_slice_in_dim(piece_up, inner, per_device, 0)
        terms = (
            lax.dot_general(
                block_normed, block_gate, contract_rows, preferred_element_type=jnp.float32
            ),
            lax.dot_general(
                block_normed, block_up, contract_rows, preferred_element_type=jnp.float32
            ),
        )
        return tuple(
            (
                total + lax.optimization_barrier(term.astype(jnp.bfloat16)).astype(jnp.float32)
                for total, term in zip(running, terms)
            )
        )

    sum_gate, sum_up = lax.fori_loop(
        0, piece_gate.shape[0] // per_device, one_block, (empty, empty)
    )
    return (
        grad_tokens.astype(jnp.bfloat16),
        grad_gain,
        sum_gate.astype(jnp.bfloat16),
        sum_up.astype(jnp.bfloat16),
    )


def solution(mesh):
    in_specs = (
        P("dp", "section"),
        P("dp", ("tp", "section")),
        P(),
        P("dp", ("tp", "section")),
        P("dp", ("tp", "section")),
    )
    out_specs = (
        P("dp", ("tp", "section")),
        P(("tp", "section")),
        P("dp", ("tp", "section")),
        P("dp", ("tp", "section")),
    )
    return jax.shard_map(shards, mesh=mesh, in_specs=in_specs, out_specs=out_specs, check_vma=False)
```

profile of v0, /device:TPU:0, one launch (start us, length us, event | category | flops | bytes accessed | tf_op | source)
XLA Modules:
  0.0 266.3 jit_solution(6498756828406113752)
XLA Ops:
  7.2 0.0 copy-start.3
  7.2 0.0 copy-start.4
  7.2 0.0 all-gather.5.cloned.1.call-start
  7.2 0.7 all-gather.5.cloned.1.call-update
  7.9 0.0 copy-start.2
  7.9 0.0 all-gather.3.cloned.1.call-start
  8.0 0.7 all-gather.3.cloned.1.call-update
  8.7 0.0 copy-done.3
  8.7 9.0 %all_gather.15 = bf16[128,2304]{0,1:T(8,128)(2,1)S(1)} all-gather(bf16[128,576]{0,1:T(8,128)(2,1)S(1)} %copy-done.3), channel_id=1, replica_groups=mesh['dp'=2,'tp'=4,'section'=4] {'section'}, dimensions={1}, use_global_device_ids=true | all-gather | bytes 737280 | tf_op jit(solution)/shard_map/all_gather | solution.py:15
  17.7 0.3 multiply_reduce_fusion
  18.1 0.0 copy-done.4
  18.1 0.4 multiply_convert_fusion
  18.4 1.1 copy.13
  19.5 3.5 %all-to-all-start = ((bf16[128,2,1152]{2,0,1:T(8,128)(2,1)}), bf16[128,2,1152]{2,0,1:T(8,128)(2,1)S(1)}, u32[]{:S(2)}, u32[]{:S(2)}) async-start(bf16[128,2,1152]{2,0,1:T(8,128)(2,1)} %copy.13), calls=%async_computation | async-start | bytes 1179648 | tf_op jit(solution)/shard_map/all_to_all | solution.py:51
  23.0 0.0 reduce-scatter.4.cloned.1.call-start
  23.1 1.1 convert_element_type.59
  24.2 0.1 dynamic_slice.27
  24.3 63.6 %all-gather.5.cloned.1.call-done = bf16[2304,1152]{1,0:T(8,128)(2,1)} async-done(((bf16[1152,1152]{1,0:T(8,128)(2,1)}), bf16[2304,1152]{1,0:T(8,128)(2,1)}) %all-gather.5.cloned.1.call-update) | async-done | bytes 5308432 | tf_op jit(solution)/shard_map/all_gather | solution.py:20
  87.9 0.0 copy-done.2
  87.9 0.0 slice-start
  87.9 3.7 %fusion.8 = (bf16[128,1152]{1,0:T(8,128)(2,1)S(1)}, f32[128,1152]{1,0:T(8,128)S(1)}) fusion(bf16[128,1152]{1,0:T(8,128)(2,1)S(1)} %copy-done.2, bf16[128,2304]{0,1:T(8,128)(2,1)S(1)} %multiply_convert_fusion, bf16[2304,1152]{1,0:T(8,128)(2,1)} %all-gather.5.cloned.1.call-done), kind=kOutput, calls=%fused_computation.19 | convolution fusion | flops 681099264 | bytes 7077888 | tf_op jit(solution)/shard_map/dot_general | solution.py:23
  91.6 67.1 %all-gather.3.cloned.1.call-done = bf16[2304,1152]{1,0:T(8,128)(2,1)} async-done(((bf16[1152,1152]{1,0:T(8,128)(2,1)}), bf16[2304,1152]{1,0:T(8,128)(2,1)}) %all-gather.3.cloned.1.call-update) | async-done | bytes 5308432 | tf_op jit(solution)/shard_map/all_gather | solution.py:21
  158.7 0.0 slice-start.1
  158.7 4.0 %fusion.15 = bf16[128,1152]{1,0:T(8,128)(2,1)S(1)} fusion(f32[128,1152]{1,0:T(8,128)S(1)} %get-tuple-element.158, bf16[128,2304]{0,1:T(8,128)(2,1)S(1)} %multiply_convert_fusion, bf16[2304,1152]{1,0:T(8,128)(2,1)} %all-gather.3.cloned.1.call-done, bf16[128,1152]{1,0:T(8,128)(2,1)} %param.8), kind=kOutput, calls=%fused_computation.26 | convolution fusion | flops 682721280 | bytes 7077888 | tf_op jit(solution)/shard_map/dot_general | solution.py:24
  162.7 0.0 slice-done
  162.7 0.0 slice-done.1
  162.7 0.0 copy-start.1
  162.7 1.6 fusion.23
  164.3 0.9 copy-done.1
  165.2 1.6 fusion.7
  166.8 1.1 copy.14
  167.9 0.0 reduce-scatter.4.cloned.1.call-update
  167.9 9.3 %all_gather.19 = bf16[256,1152]{1,0:T(8,128)(2,1)} all-gather(bf16[128,1152]{1,0:T(8,128)(2,1)S(1)} %get-tuple-element.157), channel_id=1, replica_groups=mesh['dp'=2,'tp'=4,'section'=4] {'dp'}, dimensions={0}, use_global_device_ids=true | all-gather | bytes 884736 | tf_op jit(solution)/shard_map/all_gather | solution.py:55
  177.2 8.5 %all_gather.18 = bf16[256,1152]{1,0:T(8,128)(2,1)} all-gather(bf16[128,1152]{1,0:T(8,128)(2,1)S(1)} %fusion.15), channel_id=1, replica_groups=mesh['dp'=2,'tp'=4,'section'=4] {'dp'}, dimensions={0}, use_global_device_ids=true | all-gather | bytes 884736 | tf_op jit(solution)/shard_map/all_gather | solution.py:54
  185.7 0.0 all-to-all-done
  185.7 27.0 %while.16 = (s32[]{:T(128)}, f32[1152,1152]{1,0:T(8,128)}, f32[1152,1152]{1,0:T(8,128)}, bf16[256,1152]{1,0:T(8,128)(2,1)S(1)}, bf16[256,1152]{1,0:T(8,128)(2,1)...) while((s32[]{:T(128)}, f32[1152,1152]{1,0:T(8,128)}, ...), condition=%wide.region_7.0_spmd.clone, body=%wide.region_6.0_spmd.clone.sunk | while | flops 690094080 | bytes 33032356 | solution.py:77
  185.7 1.8 convolution_convert_fusion.4
  187.6 3.4 %convolution_convert_fusion.5 = bf16[1152,1152]{1,0:T(8,128)(2,1)} fusion(bf16[256,1152]{1,0:T(8,128)(2,1)} %get-tuple-element.224, s32[]{:T(128)S(6)} %select_n.16, bf16[256,1152]{1,0:T(8,128)(2,1)S(1)} %get-tuple-element.223), kind=kOutput, calls=%fused_computation.1.clone.1 | convolution fusion | flops 341065728 | bytes 3245056 | tf_op jit(solution)/shard_map/while/body/eval_jaxpr/dot_general | solution.py:63
  190.9 6.7 %select_add_fusion.3 = (f32[1152,1152]{1,0:T(8,128)}, f32[1152,1152]{1,0:T(8,128)}) fusion(f32[1152,1152]{1,0:T(8,128)} %get-tuple-element.212, bf16[1152,1152]{1,0:T(8,128)(2,1)S(1)} %convolution_convert_fusion.4, pred[]{:T(512)S(6)} %compare.3, bf16[1152,1152]{1,0:T(8,128)(2,1)} %convolution_convert_fusion.5, f32[1152,1152]{1,0:T(8,128)} %get-tuple-element.211), kind=kLoop, calls=%fused_computation.2.clone.1 | loop fusion | flops 7962624 | bytes 26542080 | tf_op jit(solution)/shard_map/while/body/eval_jaxpr/add | solution.py:72
  197.6 1.8 convolution_convert_fusion.4
  199.5 3.4 %convolution_convert_fusion.5 = bf16[1152,1152]{1,0:T(8,128)(2,1)} fusion(bf16[256,1152]{1,0:T(8,128)(2,1)} %get-tuple-element.224, s32[]{:T(128)S(6)} %select_n.16, bf16[256,1152]{1,0:T(8,128)(2,1)S(1)} %get-tuple-element.223), kind=kOutput, calls=%fused_computation.1.clone.1 | convolution fusion | flops 341065728 | bytes 3245056 | tf_op jit(solution)/shard_map/while/body/eval_jaxpr/dot_general | solution.py:63
  202.8 9.9 %select_add_fusion.3 = (f32[1152,1152]{1,0:T(8,128)}, f32[1152,1152]{1,0:T(8,128)}) fusion(f32[1152,1152]{1,0:T(8,128)} %get-tuple-element.212, bf16[1152,1152]{1,0:T(8,128)(2,1)S(1)} %convolution_convert_fusion.4, pred[]{:T(512)S(6)} %compare.3, bf16[1152,1152]{1,0:T(8,128)(2,1)} %convolution_convert_fusion.5, f32[1152,1152]{1,0:T(8,128)} %get-tuple-element.211), kind=kLoop, calls=%fused_computation.2.clone.1 | loop fusion | flops 7962624 | bytes 26542080 | tf_op jit(solution)/shard_map/while/body/eval_jaxpr/add | solution.py:72
  212.7 0.0 copy-start
  212.7 4.4 %convert_element_type.68 = bf16[1152,1152]{1,0:T(8,128)(2,1)} convert(f32[1152,1152]{1,0:T(8,128)} %get-tuple-element.115) | non-fusion elementwise | flops 1327104 | bytes 7962624 | tf_op jit(solution)/shard_map/convert_element_type | solution.py:84
  217.1 0.2 copy-done
  217.3 1.8 convert_element_type.67
  219.1 3.0 %reduce-scatter.4.cloned.1.call-done = bf16[144,128]{1,0:T(8,128)(2,1)} async-done(((bf16[2304,128]{1,0:T(8,128)(2,1)}), bf16[144,128]{1,0:T(8,128)(2,1)}) %reduce-scatter.4.cloned.1.call-update) | async-done | bytes 36880 | tf_op jit(solution)/shard_map/reduce_scatter | solution.py:35
  222.1 1.1 fusion.20
  223.2 5.5 %psum.15 = f32[144]{0:T(256)} all-reduce(f32[144]{0:T(256)S(1)} %get-tuple-element.141), channel_id=1, replica_groups=mesh['dp'=2,'tp'=4,'section'=4] {'dp'}, use_global_device_ids=true, to_apply=%region_5.0 | all-reduce | flops 144 | bytes 1152 | tf_op jit(solution)/shard_map/psum | solution.py:44
  228.6 29.5 %psum.14 = f32[128]{0:T(128)S(1)} all-reduce(f32[128]{0:T(128)S(1)} %get-tuple-element.142), channel_id=1, replica_groups=mesh['dp'=2,'tp'=4,'section'=4] {'tp','section'}, use_global_device_ids=true, to_apply=%region_3.0 | all-reduce | flops 128 | bytes 1024 | tf_op jit(solution)/shard_map/psum | solution.py:45
  258.1 1.6 fusion.17
  (5 shorter events, 0.0 us)
Async XLA Ops:
  7.2 1.5 copy-start.3
  7.2 10.9 %copy-start.4 = (f32[2304]{0:T(1024)S(1)}, f32[2304]{0:T(1024)}, u32[]{:S(2)}) copy-start(f32[2304]{0:T(1024)} %param.9) | copy-start | bytes 27652
  7.2 80.7 %all-gather.5.cloned.1.call-start = ((), (), s32[]{:S(2)}) async-start(), calls=%async_computation.3 | async-start | bytes 7962624 | tf_op jit(solution)/shard_map/all_gather | solution.py:20
  7.9 80.0 %copy-start.2 = (bf16[128,1152]{1,0:T(8,128)(2,1)S(1)}, bf16[128,1152]{1,0:T(8,128)(2,1)}, u32[]{:S(2)}) copy-start(bf16[128,1152]{1,0:T(8,128)(2,1)} %param.8) | copy-start | bytes 884740
  7.9 150.8 %all-gather.3.cloned.1.call-start = ((), (), s32[]{:S(2)}) async-start(), calls=%async_computation.2 | async-start | bytes 7962624 | tf_op jit(solution)/shard_map/all_gather | solution.py:21
  19.5 166.2 %all-to-all-start = ((bf16[128,2,1152]{2,0,1:T(8,128)(2,1)}), bf16[128,2,1152]{2,0,1:T(8,128)(2,1)S(1)}, u32[]{:S(2)}, u32[]{:S(2)}) async-start(bf16[128,2,1152]{2,0,1:T(8,128)(2,1)} %copy.13), calls=%async_computation | async-start | bytes 1179648 | tf_op jit(solution)/shard_map/all_to_all | solution.py:51
  23.0 199.1 %reduce-scatter.4.cloned.1.call-start = ((), (), s32[]{:S(2)}) async-start(), calls=%async_computation.4 | async-start | bytes 626688 | tf_op jit(solution)/shard_map/reduce_scatter | solution.py:35
  87.9 74.8 %slice-start = ((s8[5308416]{0:T(1024)(128)(4,1)}), s8[1114112]{0:T(1024)(128)(4,1)S(1)}, s32[]{:S(2)}) async-start(s8[5308416]{0:T(1024)(128)(4,1)} %bitcast.30), calls=%async_computation.5 | async-start | bytes 2228224
  158.7 4.0 %slice-start.1 = ((s8[5308416]{0:T(1024)(128)(4,1)}), s8[4194304]{0:T(1024)(128)(4,1)S(1)}, s32[]{:S(2)}) async-start(s8[5308416]{0:T(1024)(128)(4,1)} %bitcast.30), calls=%async_computation.6 | async-start | bytes 8388608
  162.7 2.5 copy-start.1
  212.7 4.7 %copy-start = (f32[1152,1152]{1,0:T(8,128)S(1)}, f32[1152,1152]{1,0:T(8,128)}, u32[]{:S(2)}) copy-start(f32[1152,1152]{1,0:T(8,128)} %get-tuple-element.114) | copy-start | bytes 15925252
Sparse Core Ops, SparseCore 0:
  9.5 78.3 all-gather.4
  89.4 69.2 all-gather.2
  168.0 54.0 reduce-scatter.3
where the time goes:
time: 267 us; the launch traced here: 266 us
  waiting for transfers between devices  135 us (51%)
  blocking collectives  61.8 us (23%)
  other arithmetic  27.3 us (10%)
  matrix products  21.2 us (8%)
  between operations  13.9 us (5%)
  starting transfers between devices  3.64 us (1%)
  local copies, waits for them, and re-layouts  3.38 us (1%)
    all_gather x1, waiting for transfers between devices, shards(): lax.all_gather(w_up, 'dp', axis=0, tiled=True)  67.1 us
    all_gather x1, waiting for transfers between devices, shards(): lax.all_gather(w_gate, 'dp', axis=0, tiled=True)  63.6 us
    psum x1, blocking collectives, shards(): row_sum = lax.psum(row_part, ('tp', 'section'))  29.5 us
    add x2, other arithmetic, one_block(): total + lax.optimization_barrier(term.astype(jnp.bfloat16)).astype(jnp.fl...  16.6 us
    all_gather x1, blocking collectives, shards(): piece_up = lax.all_gather(d_up, 'dp', axis=0, tiled=True)  9.34 us
    all_gather x1, blocking collectives, shards(): rows_in = lax.all_gather(tokens, 'section', axis=1, tiled=True)  9.03 us
    all_gather x1, blocking collectives, shards(): piece_gate = lax.all_gather(d_gate, 'dp', axis=0, tiled=True)  8.47 us
    dot_general x2, matrix products, one_block(): lax.dot_general(block_normed, block_gate, contract_rows, preferred_elemen...  6.71 us
  transfers between devices with their start and end apart: 4, of which 3 were waited for; matrix products, arithmetic and copies ran while one was open for 18% of the time, Pallas kernels for 0%

commit v1 on v0

--- a/solution.py
+++ b/solution.py
@@ -17,7 +17,11 @@
     inv_rms = lax.rsqrt(jnp.mean(inputs * inputs, axis=1) + epsilon)
     normed = (inputs * inv_rms[:, None] * norm_gain).astype(jnp.bfloat16)
     full_gate, full_up = (
-        lax.all_gather(w_gate, "dp", axis=0, tiled=True),
+        jnp.roll(
+            jnp.concatenate([w_gate, lax.ppermute(w_gate, "dp", [(0, 1), (1, 0)])], axis=0),
+            lax.axis_index("dp") * w_gate.shape[0],
+            axis=0,
+        ),
         lax.all_gather(w_up, "dp", axis=0, tiled=True),
     )
     gate = jnp.dot(normed, full_gate, preferred_element_type=jnp.float32)

time: 267 us -> 268 us (level)
  other arithmetic: 27.3 us -> 39.4 us
  waiting for transfers between devices: 135 us -> 124 us
  blocking collectives: 61.8 us -> 58.4 us
  starting transfers between devices: 3.64 us -> 6.63 us
    all_to_all x1, waiting for transfers between devices: 0.01 us -> 101 us  [shards(): lax.all_to_all(normed, 'dp', split_axis=1, concat_axis=0, tiled=True)]
    all_gather x1, waiting for transfers between devices: 67.1 us -> 0.01 us  [shards(): lax.all_gather(w_up, 'dp', axis=0, tiled=True)]
    all_gather x1 -> x0, waiting for transfers between devices: 63.6 us -> none  [shards(): lax.all_gather(w_gate, 'dp', axis=0, tiled=True)]
    reduce_scatter x1, waiting for transfers between devices: 2.99 us -> 22.6 us  [shards(): lax.psum_scatter((first + second).astype(jnp.bfloat16), ('tp', 'section')...]
    concatenate x0 -> x1, other arithmetic: none -> 10.5 us  [shards(): jnp.roll(jnp.concatenate([w_gate, lax.ppermute(w_gate, 'dp', [(0, 1), (1,...]
    ppermute x0 -> x1, starting transfers between devices: none -> 3.03 us  [shards(): lax.ppermute(w_gate, 'dp', [(0, 1), (1, 0)])]
  transfers between devices with their start and end apart: 4 -> 4, of which waited for: 3 -> 2; matrix products, arithmetic and copies ran while one was open for 18% -> 19% of each run, Pallas kernels for 0% -> 0%
where the time goes in v1:
time: 268 us; the launch traced here: 267 us
  waiting for transfers between devices  124 us (46%)
  blocking collectives  58.4 us (22%)
  other arithmetic  39.4 us (15%)
  matrix products  20.7 us (8%)
  between operations  14.2 us (5%)
  starting transfers between devices  6.63 us (2%)
  local copies, waits for them, and re-layouts  3.52 us (1%)
    all_to_all x1, waiting for transfers between devices, shards(): lax.all_to_all(normed, 'dp', split_axis=1, concat_axis=0, tiled=True)  101 us
    psum x1, blocking collectives, shards(): row_sum = lax.psum(row_part, ('tp', 'section'))  29.5 us
    reduce_scatter x1, waiting for transfers between devices, shards(): lax.psum_scatter((first + second).astype(jnp.bfloat16), ('tp', 'section')...  22.6 us
    add x2, other arithmetic, one_block(): total + lax.optimization_barrier(term.astype(jnp.bfloat16)).astype(jnp.fl...  16.7 us
    concatenate x1, other arithmetic, shards(): jnp.roll(jnp.concatenate([w_gate, lax.ppermute(w_gate, 'dp', [(0, 1), (1,...  10.5 us
    all_gather x1, blocking collectives, shards(): piece_up = lax.all_gather(d_up, 'dp', axis=0, tiled=True)  7.84 us
    all_gather x1, blocking collectives, shards(): piece_gate = lax.all_gather(d_gate, 'dp', axis=0, tiled=True)  7.81 us
    all_gather x1, blocking collectives, shards(): rows_in = lax.all_gather(tokens, 'section', axis=1, tiled=True)  7.75 us
  transfers between devices with their start and end apart: 4, of which 2 were waited for; matrix products, arithmetic and copies ran while one was open for 19% of the time, Pallas kernels for 0%

profile of v1, /device:TPU:0, one launch (start us, length us, event | category | flops | bytes accessed | tf_op | source)
XLA Modules:
  0.0 267.2 jit_solution(6971587140816017058)
XLA Ops:
  7.2 0.0 all-gather.2.cloned.1.call-start
  7.2 0.7 all-gather.2.cloned.1.call-update
  7.9 3.0 %collective-permute-start = (bf16[1152,1152]{1,0:T(8,128)(2,1)}, bf16[1152,1152]{1,0:T(8,128)(2,1)}, u32[]{:S(2)}, u32[]{:S(2)}) collective-permute-start(bf16[1152,1152]{1,0:T(8,128)(2,1)} %param.10), channel_id=1, source_target_pairs={{0,16},{16,0},{1,17},{17,1},{2,18},{18,2},{3,19},{19,3},{4,20},{20... | collective-permute-start | bytes 7962632 | tf_op jit(solution)/shard_map/ppermute | solution.py:21
  10.9 7.8 %all_gather.12 = bf16[128,2304]{0,1:T(8,128)(2,1)S(1)} all-gather(bf16[128,576]{0,1:T(8,128)(2,1)} %param.7), channel_id=1, replica_groups=mesh['dp'=2,'tp'=4,'section'=4] {'section'}, dimensions={1}, use_global_device_ids=true | all-gather | bytes 737280 | tf_op jit(solution)/shard_map/all_gather | solution.py:15
  18.7 0.3 multiply_reduce_fusion
  19.0 1.9 multiply_convert_fusion
  20.9 3.5 %all-to-all-start = ((bf16[128,2,1152]{0,2,1:T(8,128)(2,1)}), bf16[128,2,1152]{0,2,1:T(8,128)(2,1)S(1)}, u32[]{:S(2)}, u32[]{:S(2)}) async-start(bf16[128,2,1152]{0,2,1:T(8,128)(2,1)} %bitcast.2), calls=%async_computation.1 | async-start | bytes 1179648 | tf_op jit(solution)/shard_map/all_to_all | solution.py:55
  24.4 0.0 reduce-scatter.2.cloned.1.call-start
  24.5 1.1 convert_element_type.56
  25.6 0.8 dynamic_slice.31
  26.4 101.1 %all-to-all-done = bf16[128,2,1152]{0,2,1:T(8,128)(2,1)S(1)} async-done(((bf16[128,2,1152]{0,2,1:T(8,128)(2,1)}), bf16[128,2,1152]{0,2,1:T(8,128)(2,1)S(1)}, u32[]{:S(2)}, u32[]{:S(2)}) %all-to-all-start) | async-done | bytes 589856 | tf_op jit(solution)/shard_map/all_to_all | solution.py:55
  127.5 0.3 copy.10
  127.8 0.0 copy-start.3
  127.8 0.0 collective-permute-done
  127.9 10.5 %fusion.8 = bf16[2304,1152]{1,0:T(8,128)(2,1)S(1)} fusion(s32[]{:T(128)S(6)} %select_n.28, bf16[1152,1152]{1,0:T(8,128)(2,1)} %param.10, bf16[1152,1152]{1,0:T(8,128)(2,1)} %collective-permute-done), kind=kLoop, calls=%fused_computation.16 | loop fusion | flops 21233664 | bytes 10616836 | tf_op jit(solution)/shard_map/jit(_roll_dynamic)/concatenate | solution.py:20
  138.3 0.0 copy-start.2
  138.3 2.3 copy-done.2
  140.6 0.0 copy-done.3
  140.6 2.2 fusion.10
  142.8 7.8 %all_gather.15 = bf16[256,1152]{1,0:T(8,128)(2,1)} all-gather(bf16[128,1152]{1,0:T(8,128)(2,1)S(1)} %get-tuple-element.153), channel_id=1, replica_groups=mesh['dp'=2,'tp'=4,'section'=4] {'dp'}, dimensions={0}, use_global_device_ids=true | all-gather | bytes 884736 | tf_op jit(solution)/shard_map/all_gather | solution.py:59
  150.7 0.0 all-gather.2.cloned.1.call-done
  150.7 0.0 copy-start.1
  150.7 4.1 %fusion.17 = bf16[128,1152]{1,0:T(8,128)(2,1)S(1)} fusion(f32[128,1152]{1,0:T(8,128)S(1)} %get-tuple-element.154, bf16[128,2304]{0,1:T(8,128)(2,1)} %multiply_convert_fusion, bf16[2304,1152]{1,0:T(8,128)(2,1)} %all-gather.2.cloned.1.call-done, bf16[128,1152]{1,0:T(8,128)(2,1)S(1)} %copy-done.3), kind=kOutput, calls=%fused_computation.33 | convolution fusion | flops 682721280 | bytes 7077888 | tf_op jit(solution)/shard_map/dot_general | solution.py:28
  154.8 0.0 slice-start
  154.8 7.8 %all_gather.14 = bf16[256,1152]{1,0:T(8,128)(2,1)} all-gather(bf16[128,1152]{1,0:T(8,128)(2,1)S(1)} %fusion.17), channel_id=1, replica_groups=mesh['dp'=2,'tp'=4,'section'=4] {'dp'}, dimensions={0}, use_global_device_ids=true | all-gather | bytes 884736 | tf_op jit(solution)/shard_map/all_gather | solution.py:58
  162.6 0.0 copy-done.1
  162.6 0.0 slice-start.1
  162.6 1.6 convolution_bitcast_fusion
  164.2 0.0 slice-done
  164.2 0.0 slice-done.1
  164.2 2.4 fusion.9
  166.6 0.0 reduce-scatter.2.cloned.1.call-update
  166.6 27.2 %while.16 = (s32[]{:T(128)}, f32[1152,1152]{1,0:T(8,128)}, f32[1152,1152]{1,0:T(8,128)}, bf16[256,1152]{1,0:T(8,128)(2,1)S(1)}, bf16[256,1152]{1,0:T(8,128)(2,1)...) while((s32[]{:T(128)}, f32[1152,1152]{1,0:T(8,128)}, ...), condition=%wide.region_7.8_spmd.clone, body=%wide.region_6.7_spmd.clone.sunk | while | flops 690094080 | bytes 33032356 | solution.py:81
  166.6 1.9 convolution_convert_fusion.4
  168.5 3.4 %convolution_convert_fusion.5 = bf16[1152,1152]{1,0:T(8,128)(2,1)} fusion(bf16[256,1152]{1,0:T(8,128)(2,1)} %get-tuple-element.220, s32[]{:T(128)S(6)} %select_n.31, bf16[256,1152]{1,0:T(8,128)(2,1)S(1)} %get-tuple-element.219), kind=kOutput, calls=%fused_computation.1.clone.1 | convolution fusion | flops 341065728 | bytes 3245056 | tf_op jit(solution)/shard_map/while/body/eval_jaxpr/dot_general | solution.py:67
  171.8 6.8 %select_add_fusion.3 = (f32[1152,1152]{1,0:T(8,128)}, f32[1152,1152]{1,0:T(8,128)}) fusion(f32[1152,1152]{1,0:T(8,128)} %get-tuple-element.208, bf16[1152,1152]{1,0:T(8,128)(2,1)S(1)} %convolution_convert_fusion.4, pred[]{:T(512)S(6)} %compare.3, bf16[1152,1152]{1,0:T(8,128)(2,1)} %convolution_convert_fusion.5, f32[1152,1152]{1,0:T(8,128)} %get-tuple-element.207), kind=kLoop, calls=%fused_computation.2.clone.1 | loop fusion | flops 7962624 | bytes 26542080 | tf_op jit(solution)/shard_map/while/body/eval_jaxpr/add | solution.py:76
  178.7 1.8 convolution_convert_fusion.4
  180.5 3.4 %convolution_convert_fusion.5 = bf16[1152,1152]{1,0:T(8,128)(2,1)} fusion(bf16[256,1152]{1,0:T(8,128)(2,1)} %get-tuple-element.220, s32[]{:T(128)S(6)} %select_n.31, bf16[256,1152]{1,0:T(8,128)(2,1)S(1)} %get-tuple-element.219), kind=kOutput, calls=%fused_computation.1.clone.1 | convolution fusion | flops 341065728 | bytes 3245056 | tf_op jit(solution)/shard_map/while/body/eval_jaxpr/dot_general | solution.py:67
  183.9 9.9 %select_add_fusion.3 = (f32[1152,1152]{1,0:T(8,128)}, f32[1152,1152]{1,0:T(8,128)}) fusion(f32[1152,1152]{1,0:T(8,128)} %get-tuple-element.208, bf16[1152,1152]{1,0:T(8,128)(2,1)S(1)} %convolution_convert_fusion.4, pred[]{:T(512)S(6)} %compare.3, bf16[1152,1152]{1,0:T(8,128)(2,1)} %convolution_convert_fusion.5, f32[1152,1152]{1,0:T(8,128)} %get-tuple-element.207), kind=kLoop, calls=%fused_computation.2.clone.1 | loop fusion | flops 7962624 | bytes 26542080 | tf_op jit(solution)/shard_map/while/body/eval_jaxpr/add | solution.py:76
  193.8 0.0 copy-start
  193.8 4.4 %convert_element_type.64 = bf16[1152,1152]{1,0:T(8,128)(2,1)} convert(f32[1152,1152]{1,0:T(8,128)} %get-tuple-element.115) | non-fusion elementwise | flops 1327104 | bytes 7962624 | tf_op jit(solution)/shard_map/convert_element_type | solution.py:88
  198.2 0.1 copy-done
  198.4 1.8 convert_element_type.63
  200.1 22.6 %reduce-scatter.2.cloned.1.call-done = bf16[144,128]{1,0:T(8,128)(2,1)} async-done(((bf16[2304,128]{1,0:T(8,128)(2,1)}), bf16[144,128]{1,0:T(8,128)(2,1)}) %reduce-scatter.2.cloned.1.call-update) | async-done | bytes 36880 | tf_op jit(solution)/shard_map/reduce_scatter | solution.py:39
  222.8 1.1 fusion.22
  223.8 5.5 %psum.15 = f32[144]{0:T(256)} all-reduce(f32[144]{0:T(256)S(1)} %get-tuple-element.137), channel_id=1, replica_groups=mesh['dp'=2,'tp'=4,'section'=4] {'dp'}, use_global_device_ids=true, to_apply=%region_5.6 | all-reduce | flops 144 | bytes 1152 | tf_op jit(solution)/shard_map/psum | solution.py:48
  229.3 29.5 %psum.14 = f32[128]{0:T(128)S(1)} all-reduce(f32[128]{0:T(128)S(1)} %get-tuple-element.138), channel_id=1, replica_groups=mesh['dp'=2,'tp'=4,'section'=4] {'tp','section'}, use_global_device_ids=true, to_apply=%region_3.4 | all-reduce | flops 128 | bytes 1024 | tf_op jit(solution)/shard_map/psum | solution.py:49
  258.8 1.6 fusion.19
  (5 shorter events, 0.0 us)
Async XLA Ops:
  7.2 143.5 %all-gather.2.cloned.1.call-start = ((), (), s32[]{:S(2)}) async-start(), calls=%async_computation.2 | async-start | bytes 7962624 | tf_op jit(solution)/shard_map/all_gather | solution.py:25
  7.9 119.9 %collective-permute-start = (bf16[1152,1152]{1,0:T(8,128)(2,1)}, bf16[1152,1152]{1,0:T(8,128)(2,1)}, u32[]{:S(2)}, u32[]{:S(2)}) collective-permute-start(bf16[1152,1152]{1,0:T(8,128)(2,1)} %param.10), channel_id=1, source_target_pairs={{0,16},{16,0},{1,17},{17,1},{2,18},{18,2},{3,19},{19,3},{4,20},{20... | collective-permute-start | bytes 7962632 | tf_op jit(solution)/shard_map/ppermute | solution.py:21
  20.9 106.6 %all-to-all-start = ((bf16[128,2,1152]{0,2,1:T(8,128)(2,1)}), bf16[128,2,1152]{0,2,1:T(8,128)(2,1)S(1)}, u32[]{:S(2)}, u32[]{:S(2)}) async-start(bf16[128,2,1152]{0,2,1:T(8,128)(2,1)} %bitcast.2), calls=%async_computation.1 | async-start | bytes 1179648 | tf_op jit(solution)/shard_map/all_to_all | solution.py:55
  24.4 198.3 %reduce-scatter.2.cloned.1.call-start = ((), (), s32[]{:S(2)}) async-start(), calls=%async_computation.3 | async-start | bytes 626688 | tf_op jit(solution)/shard_map/reduce_scatter | solution.py:39
  127.8 12.8 %copy-start.3 = (bf16[128,1152]{1,0:T(8,128)(2,1)S(1)}, bf16[128,1152]{1,0:T(8,128)(2,1)}, u32[]{:S(2)}) copy-start(bf16[128,1152]{1,0:T(8,128)(2,1)} %param.8) | copy-start | bytes 884740
  138.3 2.3 copy-start.2
  150.7 11.9 %copy-start.1 = (bf16[2304,1152]{1,0:T(8,128)(2,1)S(1)}, bf16[2304,1152]{1,0:T(8,128)(2,1)}, u32[]{:S(2)}) copy-start(bf16[2304,1152]{1,0:T(8,128)(2,1)} %all-gather.2.cloned.1.call-done) | copy-start | bytes 15925252
  154.8 9.4 %slice-start = ((s8[5308416]{0:T(1024)(128)(4,1)}), s8[4194304]{0:T(1024)(128)(4,1)S(1)}, s32[]{:S(2)}) async-start(s8[5308416]{0:T(1024)(128)(4,1)} %bitcast.27), calls=%async_computation.4 | async-start | bytes 8388608
  162.6 1.6 slice-start.1
  193.8 4.6 %copy-start = (f32[1152,1152]{1,0:T(8,128)S(1)}, f32[1152,1152]{1,0:T(8,128)}, u32[]{:S(2)}) copy-start(f32[1152,1152]{1,0:T(8,128)} %get-tuple-element.114) | copy-start | bytes 15925252
Sparse Core Ops, SparseCore 0:
  9.5 122.6 all-gather.1
  166.7 55.9 reduce-scatter.1
